TPU v7x, 64 devices: a 2x2x8 block of a 4x4x8 slice. The times are simulated.
64 devices in a mesh: lev: 4 (over x, y), w: 16 (over z, core).
Axes of the slice: x: 2, y: 2, z: 8, core: 2. Of those that a mesh axis runs over, the one named last changes fastest.
The devices are a block of a 4x4x8 slice.
Arguments:
- coef: float32 [320, 2, 192, 320], P('w', None, 'lev'), parts along dimension 2
- legendre: float32 [320, 320, 320], replicated
- gauss_weight: float32 [320], replicated
Outputs:
- output 1: float32 [192, 320, 640], P('lev', 'w'), parts along dimension 0
- output 2: float32 [320, 2, 192, 320], P('w', None, 'lev'), parts along dimension 2
There are 4 independent parts. A program takes and returns all parts, laid end to end along the dimension named above; an argument that names none is the same for every part.
All inputs are finite; a program needn't handle non-finite values.
Results may differ from a plain program's by a relative error of at most 0.001.
Values sent between devices are 32-bit elements.
A program may use at most 768 MiB of HBM per device.

v0:
```python
import jax
import jax.numpy as jnp
from jax import lax
from jax.sharding import PartitionSpec as P

FULL_PREC = lax.Precision.HIGHEST


def solution(mesh):
    group_size = mesh.shape['w']

    def per_device(coef, legendre, gauss_weight):
        wave_loc = coef.shape[0]
        wave_num = wave_loc * group_size
        lat_loc = legendre.shape[2] // group_size
        dev_idx = lax.axis_index('w')
        leg_own = lax.dynamic_slice_in_dim(legendre, dev_idx * wave_loc, wave_loc, axis=0)
        wt_own = lax.dynamic_slice_in_dim(gauss_weight, dev_idx * lat_loc, lat_loc, axis=0)
        fourier = jnp.einsum('mrkl,mlj->mrkj', coef, leg_own, preferred_element_type=jnp.float32, precision=FULL_PREC)
        fourier = lax.all_to_all(fourier, 'w', 3, 0, tiled=True)
        spec = jnp.transpose(lax.complex(fourier[:, 0], fourier[:, 1]), (1, 2, 0))
        grid = jnp.fft.irfft(spec, n=2 * wave_num, axis=-1)
        square_hat = jnp.fft.rfft(grid * grid, axis=-1)[:, :, :wave_num] * wt_own[None, :, None]
        re_im = jnp.stack([jnp.real(square_hat), jnp.imag(square_hat)], axis=0)
        re_im = jnp.transpose(re_im, (3, 0, 1, 2))
        re_im = lax.all_to_all(re_im, 'w', 0, 3, tiled=True)
        spec_out = jnp.einsum('mrkj,mlj->mrkl', re_im, leg_own, preferred_element_type=jnp.float32, precision=FULL_PREC)
        return grid, spec_out

    return jax.shard_map(per_device, mesh=mesh, in_specs=(P('w', None, 'lev', None), P(None, None, None), P(None)), out_specs=(P('lev', 'w', None), P('w', None, 'lev', None)), check_vma=False)
```

profile of v0, /device:TPU:21, one launch (start us, length us, event | category | flops | bytes accessed | tf_op | source)
XLA Modules:
  0.0 447.4 jit_solution(17734466223985915027)
XLA Ops:
  2.5 11.5 %fusion.36 = f32[20,2,48,320]{3,2,1,0:T(8,128)} fusion(f32[20,2,48,320]{3,2,1,0:T(8,128)S(1)} %copy-done, f32[320,320,320]{2,1,0:T(8,128)} %param.4, s32[]{:T(128)S(6)} %select_n.4), kind=kOutput, calls=%fused_computation.50 | convolution fusion | flops 2359296000 | bytes 14745604 | tf_op jit(solution)/shard_map/mrkl,mlj->mrkj/dot_general | solution.py:19
  14.0 8.7 %copy.115 = f32[20,2,48,320]{2,1,0,3:T(2,128)} copy(f32[20,2,48,320]{3,2,1,0:T(8,128)} %fusion.36) | data formatting | bytes 4915200 | tf_op jit(solution)/shard_map/mrkl,mlj->mrkj/dot_general | solution.py:19
  22.7 14.2 %reshape.28 = f32[16,1,38400]{2,1,0:T(1,128)} reshape(f32[320,20,2,48]{3,2,1,0:T(2,128)} %bitcast.162) | data formatting | bytes 4915200
  36.9 11.3 %all-to-all-start = ((f32[16,1,38400]{2,1,0:T(1,128)}), f32[16,1,38400]{2,1,0:T(1,128)S(1)}, u32[]{:S(2)}, u32[]{:S(2)}) async-start(f32[16,1,38400]{2,1,0:T(1,128)} %reshape.28), calls=%async_computation | async-start | bytes 4915200 | tf_op jit(solution)/shard_map/all_to_all | solution.py:20
  49.0 55.3 %all-to-all-done = f32[16,1,38400]{2,1,0:T(1,128)S(1)} async-done(((f32[16,1,38400]{2,1,0:T(1,128)}), f32[16,1,38400]{2,1,0:T(1,128)S(1)}, u32[]{:S(2)}, u32[]{:S(2)}) %all-to-all-start) | async-done | bytes 2457632 | tf_op jit(solution)/shard_map/all_to_all | solution.py:20
  105.0 8.6 %reduce = f32[16,38400]{1,0:T(8,128)} reduce(f32[16,1,38400]{2,1,0:T(1,128)S(1)} %all-to-all-done, f32[]{:T(128)} %broadcast.98), dimensions={1}, to_apply=%all_to_all.24.reduce_sub_computation | reduce | bytes 4915204 | tf_op jit(solution)/shard_map/all_to_all | solution.py:20
  113.6 14.1 %reshape.29 = f32[320,20,2,48]{3,2,1,0:T(2,128)} reshape(f32[16,38400]{1,0:T(8,128)} %reduce) | data formatting | bytes 4915200
  127.7 7.8 %copy.117 = f32[16,20,2,48,20]{3,2,4,1,0:T(2,128)} copy(f32[16,20,2,48,20]{3,2,1,4,0:T(2,128)} %bitcast.163) | data formatting | bytes 4915200 | tf_op jit(solution)/shard_map/all_to_all | solution.py:20
  135.5 10.9 %fusion.157 = (f32[320,1,48,20]{2,1,3,0:T(1,128)}, f32[320,1,48,20]{2,1,3,0:T(1,128)}) fusion(f32[320,2,48,20]{2,1,3,0:T(2,128)} %bitcast.161), kind=kLoop, calls=%fused_computation.153 | loop fusion | bytes 4915200 | tf_op jit(solution)/shard_map/slice | solution.py:21
  146.3 6.0 %copy.120 = f32[320,1,48,20]{0,2,3,1:T(8,128)S(1)} copy(f32[320,1,48,20]{2,1,3,0:T(1,128)} %get-tuple-element.12) | data formatting | bytes 2457600 | tf_op jit(solution)/shard_map/slice | solution.py:21
  158.5 6.4 %copy.121 = f32[48,20,640]{0,1,2:T(8,128)} copy(f32[48,20,640]{2,0,1:T(8,128)} %select_maximum_fusion) | data formatting | bytes 4915200 | tf_op jit(solution)/shard_map/jit(fft) | solution.py:22
  164.9 6.0 %copy.118 = f32[320,1,48,20]{0,2,3,1:T(8,128)S(1)} copy(f32[320,1,48,20]{2,1,3,0:T(1,128)} %get-tuple-element.13) | data formatting | bytes 2457600 | tf_op jit(solution)/shard_map/slice | solution.py:21
  177.2 6.6 %copy.119 = f32[48,20,640]{0,1,2:T(8,128)} copy(f32[48,20,640]{2,0,1:T(8,128)} %select_maximum_fusion.1) | data formatting | bytes 4915200 | tf_op jit(solution)/shard_map/jit(fft) | solution.py:22
  183.7 9.4 %jit_fft_.456 = f32[48,20,128,5]{0,1,3,2:T(8,128)} add(f32[48,20,128,5]{0,1,3,2:T(8,128)} %bitcast.154, f32[48,20,128,5]{0,1,3,2:T(8,128)} %bitcast.158) | non-fusion elementwise | flops 614400 | bytes 7372800 | tf_op jit(solution)/shard_map/jit(fft) | solution.py:22
  193.1 13.9 %fusion.11 = f32[48,20,5,128]{3,0,2,1:T(8,128)S(1)} fusion(f32[48,20,128,5]{0,1,3,2:T(8,128)} %jit_fft_.456), kind=kOutput, calls=%fused_computation.11 | convolution fusion | flops 943783936 | bytes 4915200 | tf_op jit(solution)/shard_map/jit(fft) | solution.py:22
  207.0 14.3 %fusion.39 = f32[48,20,5,128]{3,0,2,1:T(8,128)S(1)} fusion(f32[48,20,5,128]{3,0,2,1:T(8,128)S(1)} %fusion.11, f32[48,20,128,5]{0,1,3,2:T(8,128)} %bitcast.159), kind=kOutput, calls=%fused_computation.53 | convolution fusion | flops 944414720 | bytes 7372800 | tf_op jit(solution)/shard_map/jit(fft) | solution.py:22
  221.3 11.1 %fusion.154 = (f32[48,20,128,5]{2,0,3,1:T(8,128)S(1)}, f32[48,20,128,5]{2,0,3,1:T(8,128)S(1)}, f32[48,20,128,5]{2,0,3,1:T(8,128)S(1)}) fusion(f32[128,5]{0,1:T(8,128)S(1)} %get-tuple-element.16, f32[128,5]{0,1:T(8,128)S(1)} %get-tuple-element.17, f32[48,20,5,128]{3,0,2,1:T(8,128)S(1)} %fusion.39, f32[48,20,5,128]{3,0,2,1:T(8,128)S(1)} %fusion.11, ...), kind=kOutput, calls=%fused_computation.152 | convolution fusion | flops 948715520 | bytes 14750720 | tf_op jit(solution)/shard_map/jit(fft) | solution.py:22
  245.9 6.4 %bitcast_multiply_fusion.4 = (f32[48,20,5,128]{3,0,2,1:T(8,128)S(1)}, f32[48,20,128,5]{2,0,3,1:T(8,128)}) fusion(f32[48,20,128,5]{2,3,1,0:T(8,128)S(1)} %fusion.19, f32[48,20,128,5]{2,3,1,0:T(8,128)S(1)} %fusion.21, f32[48,20,128,5]{2,3,1,0:T(8,128)S(1)} %fusion.23), kind=kLoop, calls=%fused_computation.38 | loop fusion | flops 3686400 | bytes 12288000 | tf_op jit(solution)/shard_map/mul | solution.py:23
  252.3 5.0 %copy.133 = f32[48,20,5,128]{0,1,3,2:T(8,128)} copy(f32[48,20,5,128]{3,0,2,1:T(8,128)S(1)} %get-tuple-element.7) | data formatting | bytes 4915200 | tf_op jit(solution)/shard_map/mul | solution.py:23
  257.3 5.5 %copy.134 = f32[48,20,128,5]{2,0,3,1:T(8,128)S(1)} copy(f32[48,20,128,5]{0,1,3,2:T(8,128)} %bitcast.160) | data formatting | bytes 4915200 | tf_op jit(solution)/shard_map/mul | solution.py:23
  278.1 6.3 %subtract_bitcast_fusion = f32[48,20,5,128]{3,2,1,0:T(8,128)} fusion(f32[48,20,128,5]{2,3,1,0:T(8,128)S(1)} %fusion.17, f32[48,20,128,5]{2,0,3,1:T(8,128)S(1)} %get-tuple-element.5), kind=kOutput, calls=%fused_computation.26 | convolution fusion | flops 37478524 | bytes 7372800 | tf_op jit(solution)/shard_map/jit(fft) | solution.py:23
  284.4 4.7 %reshape.26 = f32[48,20,640]{2,1,0:T(8,128)} reshape(f32[48,20,5,128]{3,2,1,0:T(8,128)} %subtract_bitcast_fusion) | data formatting | bytes 4915200 | tf_op jit(solution)/shard_map/jit(fft) | solution.py:23
  290.9 7.7 %add_bitcast_fusion = f32[48,20,5,128]{3,2,1,0:T(8,128)} fusion(f32[48,20,128,5]{2,3,1,0:T(8,128)} %copy-done.2, f32[48,20,128,5]{2,0,3,1:T(8,128)S(1)} %copy-done.3), kind=kOutput, calls=%fused_computation.25 | convolution fusion | flops 37478524 | bytes 7372800 | tf_op jit(solution)/shard_map/jit(fft) | solution.py:23
  298.6 4.7 %reshape.27 = f32[48,20,640]{2,1,0:T(8,128)} reshape(f32[48,20,5,128]{3,2,1,0:T(8,128)} %add_bitcast_fusion) | data formatting | bytes 4915200 | tf_op jit(solution)/shard_map/jit(fft) | solution.py:23
  306.1 6.2 %copy.141 = f32[320,2,48,20]{2,1,3,0:T(2,128)} copy(f32[320,2,48,20]{0,2,3,1:T(8,128)S(1)} %maximum_bitcast_fusion) | data formatting | bytes 4915200 | tf_op jit(solution)/shard_map/transpose | solution.py:25
  312.3 14.2 %reshape.30 = f32[16,1,38400]{2,1,0:T(1,128)} reshape(f32[320,20,2,48]{3,2,1,0:T(2,128)} %bitcast.164) | data formatting | bytes 4915200
  326.5 5.9 %all-to-all-start.1 = ((f32[16,1,38400]{2,1,0:T(1,128)}), f32[16,1,38400]{2,1,0:T(1,128)S(1)}, u32[]{:S(2)}, u32[]{:S(2)}) async-start(f32[16,1,38400]{2,1,0:T(1,128)} %reshape.30), calls=%async_computation.1 | async-start | bytes 4915200 | tf_op jit(solution)/shard_map/all_to_all | solution.py:26
  335.7 53.4 %all-to-all-done.1 = f32[16,1,38400]{2,1,0:T(1,128)S(1)} async-done(((f32[16,1,38400]{2,1,0:T(1,128)}), f32[16,1,38400]{2,1,0:T(1,128)S(1)}, u32[]{:S(2)}, u32[]{:S(2)}) %all-to-all-start.1) | async-done | bytes 2457632 | tf_op jit(solution)/shard_map/all_to_all | solution.py:26
  389.2 8.6 %reduce.1 = f32[16,38400]{1,0:T(8,128)} reduce(f32[16,1,38400]{2,1,0:T(1,128)S(1)} %all-to-all-done.1, f32[]{:T(128)} %broadcast.98), dimensions={1}, to_apply=%all_to_all.28.reduce_sub_computation | reduce | bytes 4915204 | tf_op jit(solution)/shard_map/all_to_all | solution.py:26
  397.7 13.9 %reshape.31 = f32[320,20,2,48]{3,2,1,0:T(2,128)} reshape(f32[16,38400]{1,0:T(8,128)} %reduce.1) | data formatting | bytes 4915200
  411.6 9.2 %copy.142 = f32[20,2,48,16,20]{2,1,4,3,0:T(2,128)} copy(f32[20,2,48,16,20]{2,1,4,0,3:T(2,128)} %bitcast.165) | data formatting | bytes 4915200 | tf_op jit(solution)/shard_map/all_to_all | solution.py:26
  420.9 26.1 %fusion = f32[20,2,48,320]{3,2,1,0:T(8,128)} fusion(f32[320,320,320]{2,1,0:T(8,128)} %param.4, s32[]{:T(128)S(6)} %select_n.4, f32[20,2,48,320]{2,1,3,0:T(2,128)} %bitcast.166), kind=kOutput, calls=%fused_computation | convolution fusion | flops 2359296000 | bytes 18841604 | tf_op jit(solution)/shard_map/mrkj,mlj->mrkl/dot_general | solution.py:27
  (39 shorter events, 52.0 us)
Async XLA Ops:
  0.6 1.8 copy-start
  36.9 67.5 %all-to-all-start = ((f32[16,1,38400]{2,1,0:T(1,128)}), f32[16,1,38400]{2,1,0:T(1,128)S(1)}, u32[]{:S(2)}, u32[]{:S(2)}) async-start(f32[16,1,38400]{2,1,0:T(1,128)} %reshape.28), calls=%async_computation | async-start | bytes 4915200 | tf_op jit(solution)/shard_map/all_to_all | solution.py:20
  193.1 28.2 %slice-start = ((s8[7864320]{0:T(1024)(128)(4,1)}), s8[4194304]{0:T(1024)(128)(4,1)S(1)}, s32[]{:S(2)}) async-start(s8[7864320]{0:T(1024)(128)(4,1)} %bitcast.155), calls=%async_computation.2 | async-start | bytes 8388608
  207.0 14.3 %slice-start.1 = ((s8[7864320]{0:T(1024)(128)(4,1)}), s8[3670016]{0:T(1024)(128)(4,1)S(1)}, s32[]{:S(2)}) async-start(s8[7864320]{0:T(1024)(128)(4,1)} %bitcast.155), calls=%async_computation.3 | async-start | bytes 7340032
  276.2 1.9 copy-start.2
  289.2 1.7 copy-start.3
  303.3 1.5 slice-start.2
  303.3 2.0 slice-start.3
  326.5 62.6 %all-to-all-start.1 = ((f32[16,1,38400]{2,1,0:T(1,128)}), f32[16,1,38400]{2,1,0:T(1,128)S(1)}, u32[]{:S(2)}, u32[]{:S(2)}) async-start(f32[16,1,38400]{2,1,0:T(1,128)} %reshape.30), calls=%async_computation.1 | async-start | bytes 4915200 | tf_op jit(solution)/shard_map/all_to_all | solution.py:26
  420.9 26.1 %copy-start.1 = (f32[20,2,48,320]{3,2,1,0:T(8,128)S(1)}, f32[20,2,48,320]{3,2,1,0:T(8,128)}, u32[]{:S(2)}) copy-start(f32[20,2,48,320]{3,2,1,0:T(8,128)} %param.3) | copy-start | bytes 7372804
where the time goes:
time: 455 us; the launch traced here: 447 us
  local copies, waits for them, and re-layouts  163 us (36%)
  matrix products  118 us (26%)
  waiting for transfers between devices  109 us (24%)
  other arithmetic  39.4 us (9%)
  starting transfers between devices  17.2 us (4%)
    unnamed x19, local copies, waits for them, and re-layouts  67.5 us
    all_to_all x1, waiting for transfers between devices, per_device(): fourier = lax.all_to_all(fourier, 'w', 3, 0, tiled=True)  55.3 us
    all_to_all x1, waiting for transfers between devices, per_device(): re_im = lax.all_to_all(re_im, 'w', 0, 3, tiled=True)  53.4 us
    another operation x6, matrix products, per_device(): grid = jnp.fft.irfft(spec, n=2 * wave_num, axis=-1)  52.7 us
    another operation x6, matrix products, per_device(): jnp.fft.rfft(grid * grid, axis=-1)[:, :, :wave_num] * wt_own[None, :, None]  27.5 us
    dot_general x1, matrix products, per_device(): jnp.einsum('mrkj,mlj->mrkl', re_im, leg_own, preferred_element_type=jnp.f...  26.1 us
    slice x3, local copies, waits for them, and re-layouts, per_device(): spec = jnp.transpose(lax.complex(fourier[:, 0], fourier[:, 1]), (1, 2, 0))  22.9 us
    another operation x5, local copies, waits for them, and re-layouts, per_device(): grid = jnp.fft.irfft(spec, n=2 * wave_num, axis=-1)  17.2 us
  transfers between devices with their start and end apart: 2, of which 2 were waited for; matrix products, arithmetic and copies ran while one was open for 1% of the time, Pallas kernels for 0%

commit v1 on v0

v1 whole, which is shorter than its diff:
```python
import functools

import jax
import jax.numpy as jnp
import numpy as np
from jax import lax
from jax.experimental import pallas as pl
from jax.experimental.pallas import tpu as pltpu
from jax.sharding import PartitionSpec as P

MESH = pl.DeviceIdType.MESH
F32, BF16 = jnp.float32, jnp.bfloat16

RUN_START = (0, 8, 16)
RUN_LEN = (8, 8, 4)
LEV = 16
JPACK = 4


def split(x):
    hi = x.astype(BF16)
    return hi, (x - hi.astype(F32)).astype(BF16)


def dot3(a, b, dims):
    (ah, al), (bh, bl) = a, b
    mul = functools.partial(lax.dot_general, dimension_numbers=(dims, ((), ())), preferred_element_type=F32)
    return mul(ah, bh) + mul(al, bh) + mul(ah, bl)


def fourier_matrix(wave_num, group, wave_loc):
    lon = 2 * wave_num
    slots = []
    for start, length in zip(RUN_START, RUN_LEN):
        for dev in range(group):
            slots += [dev * wave_loc + start + i for i in range(length)]
    pad = -len(slots) % 128
    wave = np.array(slots)
    phase = (np.arange(lon)[:, None] * wave[None, :]) % lon
    ang = 2.0 * np.pi * phase / lon
    blank = np.zeros((lon, pad))
    full = np.concatenate([np.cos(ang), blank, -np.sin(ang), blank], axis=1).astype(np.float32)
    hi = full.astype(jnp.bfloat16)
    lo = (full - hi.astype(np.float32)).astype(jnp.bfloat16)
    return hi, lo


def kernel(group, coef_hbm, leg_hbm, wt_ref, ehi_hbm, elo_hbm, grid_hbm, out_hbm,
           coef, leg, leg_hi, leg_lo, ehi, elo,
           ft, wa, wb, w4, wc, ra, rb, rc, xc, lhs, qhi, qlo, ha, hb, hc, sa, sb, sc, s4, bmat, grid, spec,
           load_sem, const_sem, send1, recv1, send2, recv2, grid_sem, out_sem):
    me = lax.axis_index('w')
    wave_loc, lat = coef.shape[0], leg.shape[1]
    lat_loc = lat // group
    chunks = coef.shape[2] // LEV
    lon = ehi.shape[0]
    jgs = lat_loc // JPACK
    rows80 = group * jgs
    lane = lax.broadcasted_iota(jnp.int32, (rows80, 128), 1)

    barrier = pltpu.get_barrier_semaphore()

    def greet(i, carry):
        pl.semaphore_signal(barrier, inc=1, device_id={'w': lax.rem(me + i, group)}, device_id_type=MESH)
        return carry
    lax.fori_loop(1, group, greet, 0)

    def load(m):
        a = pltpu.make_async_copy(coef_hbm.at[m], coef.at[m], load_sem.at[0, m])
        b = pltpu.make_async_copy(leg_hbm.at[me * wave_loc + m], leg.at[m], load_sem.at[1, m])
        return a, b

    def start_load(m, carry):
        a, b = load(m)
        a.start()
        b.start()
        return carry
    lax.fori_loop(0, wave_loc, start_load, 0)
    load_e = [pltpu.make_async_copy(ehi_hbm, ehi, const_sem.at[0]), pltpu.make_async_copy(elo_hbm, elo, const_sem.at[1])]
    for cp in load_e:
        cp.start()

    xc[...] = jnp.zeros_like(xc)

    def pieces(bufs, c, dev, run):
        buf = bufs[run]
        if run < 2:
            return buf.at[c, pl.ds(pl.multiple_of(dev * (8 * jgs), 8), 8 * jgs), :]
        return buf.at[c, dev]

    def send(src, dst, ssem, rsem, c, run):
        def one(i, carry):
            to = lax.rem(me + i, group)
            pltpu.make_async_remote_copy(
                pieces(src, c, to, run), pieces(dst, c, me, run), ssem.at[c, run], rsem.at[c, run],
                device_id={'w': to}, device_id_type=MESH).start()
            return carry
        lax.fori_loop(1, group, one, 0)
        if run < 2:
            at = pl.ds(pl.multiple_of(me * (8 * jgs), 8), 8 * jgs)
            dst[run][c, at, :] = src[run][c, at, :]
        else:
            dst[run][c, me] = src[run][c, me]

    def all_bytes(bufs, c, run):
        if run < 2:
            return bufs[run].at[c, pl.ds(0, (group - 1) * 8 * jgs), :]
        return bufs[run].at[c, pl.ds(0, group - 1)]

    def wait(bufs, sem, c, run):
        ref = all_bytes(bufs, c, run)
        pltpu.make_async_copy(ref, ref, sem.at[c, run]).wait()

    src1, dst1 = (wa, wb, wc), (ra, rb, rc)
    src2, dst2 = (ha, hb, hc), (sa, sb, sc)

    def inverse(m, mm, run):
        a, b = load(m)
        a.wait()
        b.wait()
        lh, ll = split(leg[m])
        leg_hi[m] = lh
        leg_lo[m] = ll
        scale = jnp.where(me * wave_loc + m == 0, 1.0 / lon, 2.0 / lon).astype(F32)
        f = dot3(split(coef[m].reshape(2 * chunks * LEV, lat)), (lh, ll), ((1,), (0,))) * scale
        ft[:, 0:2 * chunks * LEV] = f.T
        vals = [None] * chunks
        for jj in range(JPACK):
            x = ft[pl.ds(jj, rows80, stride=JPACK), :]
            rolled = {}
            for c in range(chunks):
                for r in range(2):
                    s = (LEV * ((JPACK - chunks) * r + jj - c)) % 128
                    if s not in rolled:
                        rolled[s] = x if s == 0 else pltpu.roll(x, s, 1)
                    to = r * 64 + jj * LEV
                    mask = (lane >= to) & (lane < to + LEV)
                    vals[c] = rolled[s] if vals[c] is None else jnp.where(mask, rolled[s], vals[c])
        for c in range(chunks):
            if run < 2:
                (wa, wb)[run][c, pl.ds(mm, rows80, stride=8), :] = vals[c]
            else:
                w4[c, pl.ds(mm, rows80, stride=4), :] = vals[c]

    for run in range(3):
        def body(mm, carry, run=run):
            inverse(RUN_START[run] + mm, mm, run)
            return carry
        lax.fori_loop(0, RUN_LEN[run], body, 0)
        if run == 2:
            for c in range(chunks):
                for d in range(group):
                    wc[c, d] = w4[c, 4 * jgs * d:4 * jgs * (d + 1), :]
        if run == 0:
            pl.semaphore_wait(barrier, group - 1)
        send(src1, dst1, send1, recv1, 0, run)
    for c in range(1, chunks):
        for run in range(3):
            send(src1, dst1, send1, recv1, c, run)
    for cp in load_e:
        cp.wait()

    def latitudes(c, carry):
        for run in range(3):
            wait(dst1, recv1, c, run)
        for jg in range(jgs):
            for s in range(group):
                xc[jg, 4 * s:4 * s + 4, :] = rc[c, s, 4 * jg:4 * jg + 4, :]
        rows = JPACK * LEV
        for jg in range(jgs):
            for run in range(3):
                if run < 2:
                    buf = (ra, rb)[run]
                    x = jnp.concatenate([buf[c, 8 * (jgs * s + jg):8 * (jgs * s + jg) + 8, :] for s in range(group)], axis=0)
                else:
                    x = xc[jg]
                xt = x.T
                lhs[rows * jg:rows * (jg + 1), 128 * run:128 * (run + 1)] = xt[:rows]
                lhs[rows * jg:rows * (jg + 1), 384 + 128 * run:384 + 128 * (run + 1)] = xt[rows:]
        e = (ehi[...], elo[...])
        g = dot3(split(lhs[...]), e, ((1,), (1,)))
        for j in range(lat_loc):
            gj = g[LEV * j:LEV * (j + 1), :]
            grid[pl.ds(c * LEV, LEV), j, :] = gj
            q = gj * gj * wt_ref[me * lat_loc + j]
            hi, lo = split(q)
            qhi[LEV * j:LEV * (j + 1), :] = hi
            qlo[LEV * j:LEV * (j + 1), :] = lo
        lhs[...] = dot3((qhi[...], qlo[...]), e, ((1,), (0,)))
        for jg in range(jgs):
            for run in range(3):
                a = lhs[rows * jg:rows * (jg + 1), 128 * run:128 * (run + 1)]
                b = lhs[rows * jg:rows * (jg + 1), 384 + 128 * run:384 + 128 * (run + 1)]
                h = jnp.concatenate([a, b], axis=0).T
                for s in range(group):
                    if run < 2:
                        (ha, hb)[run][c, 8 * (jgs * s + jg):8 * (jgs * s + jg) + 8, :] = h[8 * s:8 * s + 8]
                    else:
                        hc[c, s, 4 * jg:4 * jg + 4, :] = h[4 * s:4 * s + 4]
        for run in range(3):
            send(src2, dst2, send2, recv2, c, run)
        at = pl.ds(pl.multiple_of(c * LEV, LEV), LEV)
        pltpu.make_async_copy(grid.at[at], grid_hbm.at[at], grid_sem.at[c]).start()
        return carry
    lax.fori_loop(0, chunks, latitudes, 0)

    def forward(c, run, m0, mm0, src, stride):
        for mi in range(4):
            y = src[c, pl.ds(mm0 + mi, rows80, stride=stride), :] if stride == 8 else src[pl.ds(mm0 + mi, rows80, stride=stride), :]
            for jj in range(JPACK):
                s0 = (32 * mi - LEV * jj) % 128
                s1 = (32 * mi - 48 - LEV * jj) % 128
                y0 = y if s0 == 0 else pltpu.roll(y, s0, 1)
                y1 = y if s1 == 0 else pltpu.roll(y, s1, 1)
                to = 32 * mi
                v = jnp.where((lane >= to) & (lane < to + 16), y0, jnp.where((lane >= to + 16) & (lane < to + 32), y1, 0.0))
                bmat[mi, pl.ds(jj, rows80, stride=JPACK), :] = v
        acc = None
        for mi in range(4):
            t = dot3((leg_hi[m0 + mi], leg_lo[m0 + mi]), split(bmat[mi]), ((1,), (0,)))
            acc = t if acc is None else acc + t
        o = acc.T
        for mi in range(4):
            for r in range(2):
                spec[m0 + mi, r, pl.ds(pl.multiple_of(c * LEV, LEV), LEV), :] = o[32 * mi + 16 * r:32 * mi + 16 * (r + 1)]

    def out_copy(c, run):
        ms = pl.ds(RUN_START[run], RUN_LEN[run])
        at = pl.ds(pl.multiple_of(c * LEV, LEV), LEV)
        return pltpu.make_async_copy(spec.at[ms, :, at, :], out_hbm.at[ms, :, at, :], out_sem.at[c, run])

    def spectral(c, carry):
        for run in range(3):
            wait(dst2, recv2, c, run)
            if run < 2:
                def half(i, carry2, run=run):
                    forward(c, run, RUN_START[run] + 4 * i, 4 * i, (sa, sb)[run], 8)
                    return carry2
                lax.fori_loop(0, 2, half, 0)
            else:
                for s in range(group):
                    s4[4 * jgs * s:4 * jgs * (s + 1), :] = sc[c, s]
                forward(c, run, RUN_START[2], 0, s4, 4)
            out_copy(c, run).start()
        return carry
    lax.fori_loop(0, chunks, spectral, 0)

    def drain(c, carry):
        for run in range(3):
            wait(src1, send1, c, run)
            wait(src2, send2, c, run)
            out_copy(c, run).wait()
        at = pl.ds(pl.multiple_of(c * LEV, LEV), LEV)
        pltpu.make_async_copy(grid.at[at], grid_hbm.at[at], grid_sem.at[c]).wait()
        return carry
    lax.fori_loop(0, chunks, drain, 0)


def solution(mesh):
    group = mesh.shape['w']

    def per_device(coef, legendre, gauss_weight):
        wave_loc, _, levels, degrees = coef.shape
        lat = legendre.shape[2]
        lat_loc = lat // group
        wave_num = wave_loc * group
        lon = 2 * wave_num
        chunks = levels // LEV
        jgs = lat_loc // JPACK
        ehi, elo = fourier_matrix(wave_num, group, wave_loc)
        cols = ehi.shape[1]
        big = (chunks, group * jgs * 8, 128)
        small = (chunks, group, 4 * jgs, 128)
        vm = pltpu.VMEM
        any_spec = pl.BlockSpec(memory_space=pl.ANY)
        return pl.pallas_call(
            functools.partial(kernel, group),
            out_shape=(jax.ShapeDtypeStruct((levels, lat_loc, lon), F32), jax.ShapeDtypeStruct(coef.shape, F32)),
            in_specs=[any_spec, any_spec, pl.BlockSpec(memory_space=pltpu.SMEM), any_spec, any_spec],
            out_specs=(any_spec, any_spec),
            scratch_shapes=[
                vm(coef.shape, F32), vm((wave_loc, degrees, lat), F32),
                vm((wave_loc, degrees, lat), BF16), vm((wave_loc, degrees, lat), BF16),
                vm((lon, cols), BF16), vm((lon, cols), BF16),
                vm((lat, 128), F32),
                vm(big, F32), vm(big, F32), vm((chunks, group * jgs * 4, 128), F32), vm(small, F32),
                vm(big, F32), vm(big, F32), vm(small, F32),
                vm((jgs, 128, 128), F32), vm((lat_loc * LEV, cols), F32),
                vm((lat_loc * LEV, lon), BF16), vm((lat_loc * LEV, lon), BF16),
                vm(big, F32), vm(big, F32), vm(small, F32),
                vm(big, F32), vm(big, F32), vm(small, F32), vm((group * jgs * 4, 128), F32),
                vm((4, lat, 128), F32),
                vm((levels, lat_loc, lon), F32), vm(coef.shape, F32),
                pltpu.SemaphoreType.DMA((2, wave_loc)), pltpu.SemaphoreType.DMA((2,)),
                pltpu.SemaphoreType.DMA((chunks, 3)), pltpu.SemaphoreType.DMA((chunks, 3)),
                pltpu.SemaphoreType.DMA((chunks, 3)), pltpu.SemaphoreType.DMA((chunks, 3)),
                pltpu.SemaphoreType.DMA((chunks,)), pltpu.SemaphoreType.DMA((chunks, 3)),
            ],
            compiler_params=pltpu.CompilerParams(
                collective_id=0, has_side_effects=True, vmem_limit_bytes=62 * 1024 * 1024),
        )(coef, legendre, gauss_weight, jnp.asarray(ehi), jnp.asarray(elo))

    return jax.shard_map(
        per_device, mesh=mesh,
        in_specs=(P('w', None, 'lev', None), P(None, None, None), P(None)),
        out_specs=(P('lev', 'w', None), P('w', None, 'lev', None)), check_vma=False)
```

time: 455 us -> 131 us (0.29); the launches traced: 447 us -> 130 us
  local copies, waits for them, and re-layouts: 163 us -> 5.5 us
  Pallas kernels: 0 us -> 124 us
  matrix products: 118 us -> 0 us
  waiting for transfers between devices: 109 us -> 0 us
  other arithmetic: 39.4 us -> 0 us
  starting transfers between devices: 17.2 us -> 0 us
    pallas_call x0 -> x1, Pallas kernels: none -> 124 us  [per_device(): pl.pallas_call(functools.partial(kernel, group), out_shape=(jax.ShapeDtyp...]
    all_to_all x2 -> x0, waiting for transfers between devices: 109 us -> none  [the longest x1 55.3 us: per_device(): fourier = lax.all_to_all(fourier, 'w', 3, 0, tiled=True)]
    another operation x12 -> x0, matrix products: 80.2 us -> none  [the longest x6 52.7 us: per_device(): grid = jnp.fft.irfft(spec, n=2 * wave_num, axis=-1)]
    unnamed x19 -> x3, local copies, waits for them, and re-layouts: 67.5 us -> 1.6 us
    dot_general x2 -> x0, matrix products: 37.6 us -> none  [the longest x1 26.1 us: per_device(): jnp.einsum('mrkj,mlj->mrkl', re_im, leg_own, preferred_element_type=jnp.f...]
    another operation x7 -> x0, local copies, waits for them, and re-layouts: 26.6 us -> none  [the longest x5 17.2 us: per_device(): grid = jnp.fft.irfft(spec, n=2 * wave_num, axis=-1)]
    slice x7 -> x0, local copies, waits for them, and re-layouts: 24.9 us -> none  [the longest x3 22.9 us: per_device(): spec = jnp.transpose(lax.complex(fourier[:, 0], fourier[:, 1]), (1, 2, 0))]
    all_to_all x3 -> x0, local copies, waits for them, and re-layouts: 17.6 us -> none  [the longest x1 9.21 us: per_device(): re_im = lax.all_to_all(re_im, 'w', 0, 3, tiled=True)]
  transfers between devices with their start and end apart: 2 -> 0, of which waited for: 2 -> 0; matrix products, arithmetic and copies ran while one was open for 1% -> 0% of each run, Pallas kernels for 0% -> 0%
where the time goes in v1:
time: 131 us; the launch traced here: 130 us
  Pallas kernels  124 us (95%)
  local copies, waits for them, and re-layouts  5.5 us (4%)
    pallas_call x1, Pallas kernels, per_device(): pl.pallas_call(functools.partial(kernel, group), out_shape=(jax.ShapeDtyp...  124 us
    pallas_call x1, local copies, waits for them, and re-layouts, per_device(): pl.pallas_call(functools.partial(kernel, group), out_shape=(jax.ShapeDtyp...  3.9 us

profile of v1, /device:TPU:21, one launch (start us, length us, event | category | flops | bytes accessed | tf_op | source)
XLA Modules:
  0.0 130.0 jit_solution(6896824511129689795)
XLA Ops:
  0.6 123.9 %shard_map.68 = (f32[48,20,640]{2,1,0:T(8,128)}, f32[20,2,48,320]{3,2,1,0:T(8,128)}) custom-call(f32[20,2,48,320]{3,2,1,0:T(8,128)} %coef_hbm.1, f32[320,320,320]{2,1,0:T(8,128)} %leg_hbm.1, f32[320]{0:T(512)} %wt_ref.1, bf16[640,768]{1,0:T(8,128)(2,1)} %constant.4.clone.ehi_hbm, bf16[640,768]{1,0:T(8,128)(2,1)} %constant.5.clone.elo_hbm), custom_call_target="tpu_custom_call" | custom-call | tf_op jit(solution)/shard_map/pallas_call | solution.py:276
  124.5 0.0 copy-start
  124.5 3.9 %copy.7 = f32[48,20,640]{2,0,1:T(8,128)} copy(f32[48,20,640]{2,1,0:T(8,128)} %get-tuple-element.2) | data formatting | bytes 4915200 | tf_op jit(solution)/shard_map/pallas_call | solution.py:276
  128.4 0.0 copy-done
  128.4 1.6 %copy.9 = f32[20,2,48,320]{3,2,1,0:T(8,128)} copy(f32[20,2,48,320]{3,2,1,0:T(8,128)S(1)} %copy-done) | data formatting | bytes 4915200
Async XLA Ops:
  124.5 3.9 %copy-start = (f32[20,2,48,320]{3,2,1,0:T(8,128)S(1)}, f32[20,2,48,320]{3,2,1,0:T(8,128)}, u32[]{:S(2)}) copy-start(f32[20,2,48,320]{3,2,1,0:T(8,128)} %get-tuple-element.7) | copy-start | bytes 7372804

commit v2 on v1

--- a/solution.py
+++ b/solution.py
@@ -22,10 +22,21 @@
     return hi, (x - hi.astype(F32)).astype(BF16)
 
 
-def dot3(a, b, dims):
+def product(a, b, dims):
+    return lax.dot_general(a, b, dimension_numbers=(dims, ((), ())), preferred_element_type=F32)
+
+
+def dot3_rows(a, b, dims):
     (ah, al), (bh, bl) = a, b
-    mul = functools.partial(lax.dot_general, dimension_numbers=(dims, ((), ())), preferred_element_type=F32)
-    return mul(ah, bh) + mul(al, bh) + mul(ah, bl)
+    both = product(jnp.concatenate([ah, al], axis=0), bh, dims)
+    n = ah.shape[0]
+    return both[:n] + both[n:] + product(ah, bl, dims)
+
+
+def dot3_lanes(a, b):
+    (ah, al), (bh, bl) = a, b
+    both = product(ah, jnp.concatenate([bh, bl], axis=1), ((1,), (0,)))
+    return both[:, :128] + both[:, 128:] + product(al, bh, ((1,), (0,)))
 
 
 def fourier_matrix(wave_num, group, wave_loc):
@@ -45,10 +56,28 @@
     return hi, lo
 
 
-def kernel(group, coef_hbm, leg_hbm, wt_ref, ehi_hbm, elo_hbm, grid_hbm, out_hbm,
+def forward_tile(rows, table, bmat):
+    acc = None
+    for mi in range(4):
+        y = rows(mi)
+        lane = lax.broadcasted_iota(jnp.int32, y.shape, 1)
+        to = 32 * mi
+        for jj in range(JPACK):
+            s0 = (to - LEV * jj) % 128
+            s1 = (to - 48 - LEV * jj) % 128
+            y0 = y if s0 == 0 else pltpu.roll(y, s0, 1)
+            y1 = y if s1 == 0 else pltpu.roll(y, s1, 1)
+            v = jnp.where((lane >= to) & (lane < to + 16), y0, jnp.where((lane >= to + 16) & (lane < to + 32), y1, 0.0))
+            bmat[mi, pl.ds(jj, y.shape[0], stride=JPACK), :] = v
+        t = dot3_lanes(table(mi), split(bmat[mi]))
+        acc = t if acc is None else acc + t
+    return acc.T
+
+
+def kernel(group, coef_hbm, leg_hbm, wt_ref, ehi_hbm, elo_hbm, grid, spec, s4, tail_hi, tail_lo,
            coef, leg, leg_hi, leg_lo, ehi, elo,
-           ft, wa, wb, w4, wc, ra, rb, rc, xc, lhs, qhi, qlo, ha, hb, hc, sa, sb, sc, s4, bmat, grid, spec,
-           load_sem, const_sem, send1, recv1, send2, recv2, grid_sem, out_sem):
+           ft0, ft1, wa, wb, w4, wc, ra, rb, rc, xc, lhs, qhi, qlo, ha, hb, hc, sa, sb, sc, bmat,
+           load_sem, const_sem, send1, recv1, send2, recv2):
     me = lax.axis_index('w')
     wave_loc, lat = coef.shape[0], leg.shape[1]
     lat_loc = lat // group
@@ -70,16 +99,16 @@
         b = pltpu.make_async_copy(leg_hbm.at[me * wave_loc + m], leg.at[m], load_sem.at[1, m])
         return a, b
 
-    def start_load(m, carry):
-        a, b = load(m)
-        a.start()
-        b.start()
-        return carry
-    lax.fori_loop(0, wave_loc, start_load, 0)
+    def order(i):
+        return lax.rem(i + RUN_START[2], wave_loc)
+
+    def start_load(i):
+        for cp in load(order(i)):
+            cp.start()
+
+    for i in range(RUN_LEN[2]):
+        start_load(i)
     load_e = [pltpu.make_async_copy(ehi_hbm, ehi, const_sem.at[0]), pltpu.make_async_copy(elo_hbm, elo, const_sem.at[1])]
-    for cp in load_e:
-        cp.start()
-
     xc[...] = jnp.zeros_like(xc)
 
     def pieces(bufs, c, dev, run):
@@ -89,8 +118,9 @@
         return buf.at[c, dev]
 
     def send(src, dst, ssem, rsem, c, run):
-        def one(i, carry):
-            to = lax.rem(me + i, group)
+        def one(j, carry):
+            i = group - j
+            to = lax.rem(me + group + (2 * lax.rem(i, 2) - 1) * ((i + 1) // 2), group)
             pltpu.make_async_remote_copy(
                 pieces(src, c, to, run), pieces(dst, c, me, run), ssem.at[c, run], rsem.at[c, run],
                 device_id={'w': to}, device_id_type=MESH).start()
@@ -114,15 +144,16 @@
     src1, dst1 = (wa, wb, wc), (ra, rb, rc)
     src2, dst2 = (ha, hb, hc), (sa, sb, sc)
 
-    def inverse(m, mm, run):
-        a, b = load(m)
-        a.wait()
-        b.wait()
+    def inverse(m, mm, run, ft):
         lh, ll = split(leg[m])
-        leg_hi[m] = lh
-        leg_lo[m] = ll
+        if run < 2:
+            leg_hi[m] = lh
+            leg_lo[m] = ll
+        else:
+            tail_hi[mm] = lh
+            tail_lo[mm] = ll
         scale = jnp.where(me * wave_loc + m == 0, 1.0 / lon, 2.0 / lon).astype(F32)
-        f = dot3(split(coef[m].reshape(2 * chunks * LEV, lat)), (lh, ll), ((1,), (0,))) * scale
+        f = dot3_rows(split(coef[m].reshape(2 * chunks * LEV, lat)), (lh, ll), ((1,), (0,))) * scale
         ft[:, 0:2 * chunks * LEV] = f.T
         vals = [None] * chunks
         for jj in range(JPACK):
@@ -142,20 +173,34 @@
             else:
                 w4[c, pl.ds(mm, rows80, stride=4), :] = vals[c]
 
-    for run in range(3):
-        def body(mm, carry, run=run):
-            inverse(RUN_START[run] + mm, mm, run)
+    done = 0
+    for run in (2, 0, 1):
+        def pair(i, carry, run=run, done=done):
+            for k in range(2):
+                @pl.when(done + 2 * i + k + RUN_LEN[2] < wave_loc)
+                def _(k=k):
+                    start_load(done + 2 * i + k + RUN_LEN[2])
+            for k in range(2):
+                for cp in load(RUN_START[run] + 2 * i + k):
+                    cp.wait()
+            for k, ft in ((0, ft0), (1, ft1)):
+                inverse(RUN_START[run] + 2 * i + k, 2 * i + k, run, ft)
             return carry
-        lax.fori_loop(0, RUN_LEN[run], body, 0)
+        lax.fori_loop(0, RUN_LEN[run] // 2, pair, 0)
+        done += RUN_LEN[run]
         if run == 2:
+            for cp in load_e:
+                cp.start()
             for c in range(chunks):
                 for d in range(group):
                     wc[c, d] = w4[c, 4 * jgs * d:4 * jgs * (d + 1), :]
-        if run == 0:
             pl.semaphore_wait(barrier, group - 1)
-        send(src1, dst1, send1, recv1, 0, run)
+            for c in range(chunks):
+                send(src1, dst1, send1, recv1, c, run)
+        else:
+            send(src1, dst1, send1, recv1, 0, run)
     for c in range(1, chunks):
-        for run in range(3):
+        for run in range(2):
             send(src1, dst1, send1, recv1, c, run)
     for cp in load_e:
         cp.wait()
@@ -178,15 +223,15 @@
                 lhs[rows * jg:rows * (jg + 1), 128 * run:128 * (run + 1)] = xt[:rows]
                 lhs[rows * jg:rows * (jg + 1), 384 + 128 * run:384 + 128 * (run + 1)] = xt[rows:]
         e = (ehi[...], elo[...])
-        g = dot3(split(lhs[...]), e, ((1,), (1,)))
+        g = dot3_rows(split(lhs[...]), e, ((1,), (1,)))
         for j in range(lat_loc):
             gj = g[LEV * j:LEV * (j + 1), :]
-            grid[pl.ds(c * LEV, LEV), j, :] = gj
+            grid[j, pl.ds(pl.multiple_of(c * LEV, LEV), LEV), :] = gj
             q = gj * gj * wt_ref[me * lat_loc + j]
             hi, lo = split(q)
             qhi[LEV * j:LEV * (j + 1), :] = hi
             qlo[LEV * j:LEV * (j + 1), :] = lo
-        lhs[...] = dot3((qhi[...], qlo[...]), e, ((1,), (0,)))
+        lhs[...] = dot3_rows((qhi[...], qlo[...]), e, ((1,), (0,)))
         for jg in range(jgs):
             for run in range(3):
                 a = lhs[rows * jg:rows * (jg + 1), 128 * run:128 * (run + 1)]
@@ -199,49 +244,37 @@
                         hc[c, s, 4 * jg:4 * jg + 4, :] = h[4 * s:4 * s + 4]
         for run in range(3):
             send(src2, dst2, send2, recv2, c, run)
-        at = pl.ds(pl.multiple_of(c * LEV, LEV), LEV)
-        pltpu.make_async_copy(grid.at[at], grid_hbm.at[at], grid_sem.at[c]).start()
         return carry
     lax.fori_loop(0, chunks, latitudes, 0)
 
-    def forward(c, run, m0, mm0, src, stride):
-        for mi in range(4):
-            y = src[c, pl.ds(mm0 + mi, rows80, stride=stride), :] if stride == 8 else src[pl.ds(mm0 + mi, rows80, stride=stride), :]
-            for jj in range(JPACK):
-                s0 = (32 * mi - LEV * jj) % 128
-                s1 = (32 * mi - 48 - LEV * jj) % 128
-                y0 = y if s0 == 0 else pltpu.roll(y, s0, 1)
-                y1 = y if s1 == 0 else pltpu.roll(y, s1, 1)
-                to = 32 * mi
-                v = jnp.where((lane >= to) & (lane < to + 16), y0, jnp.where((lane >= to + 16) & (lane < to + 32), y1, 0.0))
-                bmat[mi, pl.ds(jj, rows80, stride=JPACK), :] = v
-        acc = None
-        for mi in range(4):
-            t = dot3((leg_hi[m0 + mi], leg_lo[m0 + mi]), split(bmat[mi]), ((1,), (0,)))
-            acc = t if acc is None else acc + t
-        o = acc.T
+    def forward(c, run, mm0):
+        m0 = RUN_START[run] + mm0
+        if run < 2:
+            rows = lambda mi: (sa, sb)[run][c, pl.ds(mm0 + mi, rows80, stride=8), :]
+            table = lambda mi: (leg_hi[m0 + mi], leg_lo[m0 + mi])
+        else:
+            rows = lambda mi: s4[pl.ds(mi, rows80, stride=4), :]
+            table = lambda mi: (tail_hi[mi], tail_lo[mi])
+        o = forward_tile(rows, table, bmat)
         for mi in range(4):
             for r in range(2):
                 spec[m0 + mi, r, pl.ds(pl.multiple_of(c * LEV, LEV), LEV), :] = o[32 * mi + 16 * r:32 * mi + 16 * (r + 1)]
-
-    def out_copy(c, run):
-        ms = pl.ds(RUN_START[run], RUN_LEN[run])
-        at = pl.ds(pl.multiple_of(c * LEV, LEV), LEV)
-        return pltpu.make_async_copy(spec.at[ms, :, at, :], out_hbm.at[ms, :, at, :], out_sem.at[c, run])
 
     def spectral(c, carry):
         for run in range(3):
             wait(dst2, recv2, c, run)
             if run < 2:
                 def half(i, carry2, run=run):
-                    forward(c, run, RUN_START[run] + 4 * i, 4 * i, (sa, sb)[run], 8)
+                    forward(c, run, 4 * i)
                     return carry2
                 lax.fori_loop(0, 2, half, 0)
             else:
                 for s in range(group):
                     s4[4 * jgs * s:4 * jgs * (s + 1), :] = sc[c, s]
-                forward(c, run, RUN_START[2], 0, s4, 4)
-            out_copy(c, run).start()
+
+                @pl.when(c < chunks - 1)
+                def _():
+                    forward(c, 2, 0)
         return carry
     lax.fori_loop(0, chunks, spectral, 0)
 
@@ -249,11 +282,33 @@
         for run in range(3):
             wait(src1, send1, c, run)
             wait(src2, send2, c, run)
-            out_copy(c, run).wait()
-        at = pl.ds(pl.multiple_of(c * LEV, LEV), LEV)
-        pltpu.make_async_copy(grid.at[at], grid_hbm.at[at], grid_sem.at[c]).wait()
         return carry
     lax.fori_loop(0, chunks, drain, 0)
+
+
+def write_out(grid, spec, last, tail_hi, tail_lo, grid_hbm, spec_hbm, bmat, piece, sem):
+    half = grid.shape[0] // 2
+    m0, left = RUN_START[2], spec.shape[2] - LEV
+    piece_hbm = spec_hbm.at[pl.ds(m0, RUN_LEN[2]), :, pl.ds(left, LEV), :]
+    copies = [
+        pltpu.make_async_copy(grid.at[pl.ds(0, half)], grid_hbm.at[pl.ds(0, half)], sem.at[0]),
+        pltpu.make_async_copy(grid.at[pl.ds(half, half)], grid_hbm.at[pl.ds(half, half)], sem.at[1]),
+        pltpu.make_async_copy(spec.at[pl.ds(0, m0 // 2)], spec_hbm.at[pl.ds(0, m0 // 2)], sem.at[2]),
+        pltpu.make_async_copy(spec.at[pl.ds(m0 // 2, m0 // 2)], spec_hbm.at[pl.ds(m0 // 2, m0 // 2)], sem.at[3]),
+        pltpu.make_async_copy(spec.at[pl.ds(m0, RUN_LEN[2]), :, pl.ds(0, left), :],
+                              spec_hbm.at[pl.ds(m0, RUN_LEN[2]), :, pl.ds(0, left), :], sem.at[4]),
+    ]
+    for cp in copies:
+        cp.start()
+    rows80 = last.shape[0] // 4
+    o = forward_tile(lambda mi: last[pl.ds(mi, rows80, stride=4), :], lambda mi: (tail_hi[mi], tail_lo[mi]), bmat)
+    for mi in range(RUN_LEN[2]):
+        for r in range(2):
+            piece[mi, r] = o[32 * mi + 16 * r:32 * mi + 16 * (r + 1)]
+    cp = pltpu.make_async_copy(piece, piece_hbm, sem.at[5])
+    cp.start()
+    for cp in copies + [cp]:
+        cp.wait()
 
 
 def solution(mesh):
@@ -273,32 +328,40 @@
         small = (chunks, group, 4 * jgs, 128)
         vm = pltpu.VMEM
         any_spec = pl.BlockSpec(memory_space=pl.ANY)
-        return pl.pallas_call(
+        grid, spec, last, tail_hi, tail_lo = pl.pallas_call(
             functools.partial(kernel, group),
-            out_shape=(jax.ShapeDtypeStruct((levels, lat_loc, lon), F32), jax.ShapeDtypeStruct(coef.shape, F32)),
+            out_shape=(vm((lat_loc, levels, lon), F32), vm(coef.shape, F32), vm((group * jgs * 4, 128), F32),
+                       vm((RUN_LEN[2], degrees, lat), BF16), vm((RUN_LEN[2], degrees, lat), BF16)),
             in_specs=[any_spec, any_spec, pl.BlockSpec(memory_space=pltpu.SMEM), any_spec, any_spec],
-            out_specs=(any_spec, any_spec),
+            out_specs=(pl.BlockSpec(memory_space=vm),) * 5,
             scratch_shapes=[
                 vm(coef.shape, F32), vm((wave_loc, degrees, lat), F32),
-                vm((wave_loc, degrees, lat), BF16), vm((wave_loc, degrees, lat), BF16),
+                vm((RUN_START[2], degrees, lat), BF16), vm((RUN_START[2], degrees, lat), BF16),
                 vm((lon, cols), BF16), vm((lon, cols), BF16),
-                vm((lat, 128), F32),
+                vm((lat, 128), F32), vm((lat, 128), F32),
                 vm(big, F32), vm(big, F32), vm((chunks, group * jgs * 4, 128), F32), vm(small, F32),
                 vm(big, F32), vm(big, F32), vm(small, F32),
                 vm((jgs, 128, 128), F32), vm((lat_loc * LEV, cols), F32),
                 vm((lat_loc * LEV, lon), BF16), vm((lat_loc * LEV, lon), BF16),
                 vm(big, F32), vm(big, F32), vm(small, F32),
-                vm(big, F32), vm(big, F32), vm(small, F32), vm((group * jgs * 4, 128), F32),
+                vm(big, F32), vm(big, F32), vm(small, F32),
                 vm((4, lat, 128), F32),
-                vm((levels, lat_loc, lon), F32), vm(coef.shape, F32),
                 pltpu.SemaphoreType.DMA((2, wave_loc)), pltpu.SemaphoreType.DMA((2,)),
                 pltpu.SemaphoreType.DMA((chunks, 3)), pltpu.SemaphoreType.DMA((chunks, 3)),
                 pltpu.SemaphoreType.DMA((chunks, 3)), pltpu.SemaphoreType.DMA((chunks, 3)),
-                pltpu.SemaphoreType.DMA((chunks,)), pltpu.SemaphoreType.DMA((chunks, 3)),
             ],
             compiler_params=pltpu.CompilerParams(
-                collective_id=0, has_side_effects=True, vmem_limit_bytes=62 * 1024 * 1024),
+                collective_id=0, has_side_effects=True, vmem_limit_bytes=50 * 1024 * 1024),
         )(coef, legendre, gauss_weight, jnp.asarray(ehi), jnp.asarray(elo))
+        grid, spec = pl.pallas_call(
+            write_out,
+            out_shape=(jax.ShapeDtypeStruct(grid.shape, F32), jax.ShapeDtypeStruct(spec.shape, F32)),
+            in_specs=[any_spec, any_spec, pl.BlockSpec(memory_space=vm), pl.BlockSpec(memory_space=vm), pl.BlockSpec(memory_space=vm)],
+            out_specs=(pl.BlockSpec(memory_space=pltpu.HBM), pl.BlockSpec(memory_space=pltpu.HBM)),
+            scratch_shapes=[vm((4, lat, 128), F32), vm((RUN_LEN[2], 2, LEV, degrees), F32), pltpu.SemaphoreType.DMA((6,))],
+            compiler_params=pltpu.CompilerParams(vmem_limit_bytes=12 * 1024 * 1024),
+        )(grid, spec, last, tail_hi, tail_lo)
+        return jnp.transpose(grid, (1, 0, 2)), spec
 
     return jax.shard_map(
         per_device, mesh=mesh,

time: 131 us -> 124 us (0.947)
  local copies, waits for them, and re-layouts: 5.5 us -> 0 us
    pallas_call x1 -> x0, local copies, waits for them, and re-layouts: 3.9 us -> none  [per_device(): pl.pallas_call(functools.partial(kernel, group), out_shape=(jax.ShapeDtyp...]
    unnamed x3 -> x0, local copies, waits for them, and re-layouts: 1.6 us -> none
    pallas_call x1 -> x2, Pallas kernels: 124 us -> 123 us  [the longest x1 120 us: per_device(): pl.pallas_call(functools.partial(kernel, group), out_shape=(vm((lat_loc,...]
where the time goes in v2:
time: 124 us; the launch traced here: 123 us
  Pallas kernels  123 us (99%)
    pallas_call x1, Pallas kernels, per_device(): pl.pallas_call(functools.partial(kernel, group), out_shape=(vm((lat_loc,...  120 us

profile of v2, /device:TPU:21, one launch (start us, length us, event | category | flops | bytes accessed | tf_op | source)
XLA Modules:
  0.0 123.1 jit_solution(15206528592784569000)
XLA Ops:
  0.6 120.1 %shard_map.68 = (f32[20,48,640]{2,1,0:T(8,128)S(1)}, f32[20,2,48,320]{3,2,1,0:T(8,128)S(1)}, f32[320,128]{1,0:T(8,128)S(1)}, bf16[4,320,320]{2,1,0:T(8,128)(2,1)S(1)}, bf16[4,320,320]{2,1,0:T(8,128)(2,1)S(1)}) custom-call(f32[20,2,48,320]{3,2,1,0:T(8,128)} %coef_hbm.1, f32[320,320,320]{2,1,0:T(8,128)} %leg_hbm.1, f32[320]{0:T(512)} %wt_ref.1, ...), custom_call_target="tpu_custom_call" | custom-call | tf_op jit(solution)/shard_map/pallas_call | solution.py:331
  120.7 2.4 %shard_map.69 = (f32[20,48,640]{2,1,0:T(8,128)}, f32[20,2,48,320]{3,2,1,0:T(8,128)}) custom-call(f32[20,48,640]{2,1,0:T(8,128)S(1)} %get-tuple-element.9.grid, f32[20,2,48,320]{3,2,1,0:T(8,128)S(1)} %get-tuple-element.10.spec, f32[320,128]{1,0:T(8,128)S(1)} %get-tuple-element.11.last, bf16[4,320,320]{2,1,0:T(8,128)(2,1)S(1)} %get-tuple-element.12.tail_hi, ...), custom_call_target="tpu_custom_call" | custom-call | tf_op jit(solution)/shard_map/pallas_call | solution.py:356

commit v3 on v2

--- a/solution.py
+++ b/solution.py
@@ -74,10 +74,10 @@
     return acc.T
 
 
-def kernel(group, coef_hbm, leg_hbm, wt_ref, ehi_hbm, elo_hbm, grid, spec, s4, tail_hi, tail_lo,
+def kernel(group, coef_hbm, leg_hbm, wt_hbm, ehi_hbm, elo_hbm, grid, spec, s4, tail_hi, tail_lo,
            coef, leg, leg_hi, leg_lo, ehi, elo,
            ft0, ft1, wa, wb, w4, wc, ra, rb, rc, xc, lhs, qhi, qlo, ha, hb, hc, sa, sb, sc, bmat,
-           load_sem, const_sem, send1, recv1, send2, recv2):
+           wt, load_sem, const_sem, send1, recv1, send2, recv2):
     me = lax.axis_index('w')
     wave_loc, lat = coef.shape[0], leg.shape[1]
     lat_loc = lat // group
@@ -89,10 +89,12 @@
 
     barrier = pltpu.get_barrier_semaphore()
 
-    def greet(i, carry):
-        pl.semaphore_signal(barrier, inc=1, device_id={'w': lax.rem(me + i, group)}, device_id_type=MESH)
-        return carry
-    lax.fori_loop(1, group, greet, 0)
+    def peer(i):
+        far = group - i
+        return lax.rem(me + group + (2 * lax.rem(far, 2) - 1) * ((far + 1) // 2), group)
+
+    for i in range(1, group):
+        pl.semaphore_signal(barrier, inc=1, device_id={'w': peer(i)}, device_id_type=MESH)
 
     def load(m):
         a = pltpu.make_async_copy(coef_hbm.at[m], coef.at[m], load_sem.at[0, m])
@@ -108,8 +110,13 @@
 
     for i in range(RUN_LEN[2]):
         start_load(i)
-    load_e = [pltpu.make_async_copy(ehi_hbm, ehi, const_sem.at[0]), pltpu.make_async_copy(elo_hbm, elo, const_sem.at[1])]
+    load_e = [pltpu.make_async_copy(ehi_hbm, ehi, const_sem.at[0]), pltpu.make_async_copy(elo_hbm, elo, const_sem.at[1]),
+              pltpu.make_async_copy(wt_hbm, wt, const_sem.at[2])]
     xc[...] = jnp.zeros_like(xc)
+
+    ring = group // 2
+    peers = [p for d in range(1, ring // 2) for p in ((d, 0), (-d, 1), (-d, 0), (d, 1))]
+    peers += [(ring // 2, 0), (ring // 2, 1), (0, 1)]
 
     def pieces(bufs, c, dev, run):
         buf = bufs[run]
@@ -118,14 +125,11 @@
         return buf.at[c, dev]
 
     def send(src, dst, ssem, rsem, c, run):
-        def one(j, carry):
-            i = group - j
-            to = lax.rem(me + group + (2 * lax.rem(i, 2) - 1) * ((i + 1) // 2), group)
+        for dist, core in peers:
+            to = lax.rem(me // 2 + dist + ring, ring) * 2 + lax.rem(me + core, 2)
             pltpu.make_async_remote_copy(
                 pieces(src, c, to, run), pieces(dst, c, me, run), ssem.at[c, run], rsem.at[c, run],
                 device_id={'w': to}, device_id_type=MESH).start()
-            return carry
-        lax.fori_loop(1, group, one, 0)
         if run < 2:
             at = pl.ds(pl.multiple_of(me * (8 * jgs), 8), 8 * jgs)
             dst[run][c, at, :] = src[run][c, at, :]
@@ -227,7 +231,7 @@
         for j in range(lat_loc):
             gj = g[LEV * j:LEV * (j + 1), :]
             grid[j, pl.ds(pl.multiple_of(c * LEV, LEV), LEV), :] = gj
-            q = gj * gj * wt_ref[me * lat_loc + j]
+            q = gj * gj * wt[me * lat_loc + j]
             hi, lo = split(q)
             qhi[LEV * j:LEV * (j + 1), :] = hi
             qlo[LEV * j:LEV * (j + 1), :] = lo
@@ -332,7 +336,7 @@
             functools.partial(kernel, group),
             out_shape=(vm((lat_loc, levels, lon), F32), vm(coef.shape, F32), vm((group * jgs * 4, 128), F32),
                        vm((RUN_LEN[2], degrees, lat), BF16), vm((RUN_LEN[2], degrees, lat), BF16)),
-            in_specs=[any_spec, any_spec, pl.BlockSpec(memory_space=pltpu.SMEM), any_spec, any_spec],
+            in_specs=[any_spec] * 5,
             out_specs=(pl.BlockSpec(memory_space=vm),) * 5,
             scratch_shapes=[
                 vm(coef.shape, F32), vm((wave_loc, degrees, lat), F32),
@@ -346,7 +350,7 @@
                 vm(big, F32), vm(big, F32), vm(small, F32),
                 vm(big, F32), vm(big, F32), vm(small, F32),
                 vm((4, lat, 128), F32),
-                pltpu.SemaphoreType.DMA((2, wave_loc)), pltpu.SemaphoreType.DMA((2,)),
+                pltpu.SMEM((lat,), F32), pltpu.SemaphoreType.DMA((2, wave_loc)), pltpu.SemaphoreType.DMA((3,)),
                 pltpu.SemaphoreType.DMA((chunks, 3)), pltpu.SemaphoreType.DMA((chunks, 3)),
                 pltpu.SemaphoreType.DMA((chunks, 3)), pltpu.SemaphoreType.DMA((chunks, 3)),
             ],

time: 124 us -> 123 us (level)
  no operation moved by 1% of the time
where the time goes in v3:
time: 123 us
  Pallas kernels  122 us (99%)
    pallas_call x1, Pallas kernels, per_device(): pl.pallas_call(functools.partial(kernel, group), out_shape=(vm((lat_loc,...  120 us

profile of v3, /device:TPU:21, one launch (start us, length us, event | category | flops | bytes accessed | tf_op | source)
XLA Modules:
  0.0 122.7 jit_solution(7143959589690290391)
XLA Ops:
  0.6 119.7 %shard_map.68 = (f32[20,48,640]{2,1,0:T(8,128)S(1)}, f32[20,2,48,320]{3,2,1,0:T(8,128)S(1)}, f32[320,128]{1,0:T(8,128)S(1)}, bf16[4,320,320]{2,1,0:T(8,128)(2,1)S(1)}, bf16[4,320,320]{2,1,0:T(8,128)(2,1)S(1)}) custom-call(f32[20,2,48,320]{3,2,1,0:T(8,128)} %coef_hbm.1, f32[320,320,320]{2,1,0:T(8,128)} %leg_hbm.1, f32[320]{0:T(512)} %wt_hbm.1, ...), custom_call_target="tpu_custom_call" | custom-call | tf_op jit(solution)/shard_map/pallas_call | solution.py:335
  120.3 2.4 %shard_map.69 = (f32[20,48,640]{2,1,0:T(8,128)}, f32[20,2,48,320]{3,2,1,0:T(8,128)}) custom-call(f32[20,48,640]{2,1,0:T(8,128)S(1)} %get-tuple-element.9.grid, f32[20,2,48,320]{3,2,1,0:T(8,128)S(1)} %get-tuple-element.10.spec, f32[320,128]{1,0:T(8,128)S(1)} %get-tuple-element.11.last, bf16[4,320,320]{2,1,0:T(8,128)(2,1)S(1)} %get-tuple-element.12.tail_hi, ...), custom_call_target="tpu_custom_call" | custom-call | tf_op jit(solution)/shard_map/pallas_call | solution.py:360

commit v4 on v3

--- a/solution.py
+++ b/solution.py
@@ -116,7 +116,7 @@
 
     ring = group // 2
     peers = [p for d in range(1, ring // 2) for p in ((d, 0), (-d, 1), (-d, 0), (d, 1))]
-    peers += [(ring // 2, 0), (ring // 2, 1), (0, 1)]
+    peers = [(0, 1)] + peers + [(ring // 2, 0), (ring // 2, 1)]
 
     def pieces(bufs, c, dev, run):
         buf = bufs[run]

time: 123 us -> 124 us (level)
  no operation moved by 1% of the time
where the time goes in v4:
time: 124 us
  Pallas kernels  123 us (99%)
    pallas_call x1, Pallas kernels, per_device(): pl.pallas_call(functools.partial(kernel, group), out_shape=(vm((lat_loc,...  121 us

profile of v4, /device:TPU:21, one launch (start us, length us, event | category | flops | bytes accessed | tf_op | source)
XLA Modules:
  0.0 123.9 jit_solution(8171647716994529974)
XLA Ops:
  0.6 120.8 %shard_map.68 = (f32[20,48,640]{2,1,0:T(8,128)S(1)}, f32[20,2,48,320]{3,2,1,0:T(8,128)S(1)}, f32[320,128]{1,0:T(8,128)S(1)}, bf16[4,320,320]{2,1,0:T(8,128)(2,1)S(1)}, bf16[4,320,320]{2,1,0:T(8,128)(2,1)S(1)}) custom-call(f32[20,2,48,320]{3,2,1,0:T(8,128)} %coef_hbm.1, f32[320,320,320]{2,1,0:T(8,128)} %leg_hbm.1, f32[320]{0:T(512)} %wt_hbm.1, ...), custom_call_target="tpu_custom_call" | custom-call | tf_op jit(solution)/shard_map/pallas_call | solution.py:335
  121.4 2.4 %shard_map.69 = (f32[20,48,640]{2,1,0:T(8,128)}, f32[20,2,48,320]{3,2,1,0:T(8,128)}) custom-call(f32[20,48,640]{2,1,0:T(8,128)S(1)} %get-tuple-element.9.grid, f32[20,2,48,320]{3,2,1,0:T(8,128)S(1)} %get-tuple-element.10.spec, f32[320,128]{1,0:T(8,128)S(1)} %get-tuple-element.11.last, bf16[4,320,320]{2,1,0:T(8,128)(2,1)S(1)} %get-tuple-element.12.tail_hi, ...), custom_call_target="tpu_custom_call" | custom-call | tf_op jit(solution)/shard_map/pallas_call | solution.py:360
